TPU v7x, 32 devices: a whole 2x2x4 slice. The times are simulated.
32 devices in a mesh: tile: 8 (over z, x), sub: 4 (over y, core).
Axes of the slice: x: 2, y: 2, z: 4, core: 2. Of those that a mesh axis runs over, the one named last changes fastest.
Arguments:
- initial_state: float32 [8, 64, 1024], P('tile', None, 'sub'), may hold values from -6 to 6
- cotangent: float32 [8, 64, 1024], P('tile', None, 'sub'), may hold values from -6 to 6
- w_in: bfloat16 [576, 1024], replicated, may hold values from -0.25 to 0.25
- b_in: float32 [1024], replicated, may hold values from -3 to 3
- w_out: bfloat16 [64, 1024], replicated, may hold values from -0.1875 to 0.1875
- edge_flips: int32 [8, 2], P('tile'), may hold values 0 or 1
Outputs:
- final_state: float32 [8, 64, 1024], P('tile', None, 'sub')
- grad_state: float32 [8, 64, 1024], P('tile', None, 'sub')
- grad_w_in: float32 [576, 1024], replicated
- grad_b_in: float32 [1024], replicated
- grad_w_out: float32 [64, 1024], replicated
All inputs are finite; a program needn't handle non-finite values. No bound on the sum of `edge_flips` on one device may be relied on, other than what follows from the above.
Results may differ from a plain program's by a relative error of at most 0.006.
Values may be sent and summed in bfloat16 or wider, within the bound.
A program may use at most 64 MiB of HBM per device.

v0:
```python
import jax
import jax.numpy as jnp
from jax import lax
from jax.sharding import PartitionSpec as P

LEVELS = 64
ROWS = 8
STEPS = 4
TILE_ROW = 4
STEP_SIZE = 0.25


def from_behind(value, axis, by):
    peers = lax.axis_size(axis)
    return lax.ppermute(value, axis, [(i, (i + by) % peers) for i in range(peers)])


def passed_along(value, axis, steps):
    count = lax.axis_size(axis)
    first, last = (max(0, -steps), min(count, count - steps))
    return lax.ppermute(value, axis, [(source, source + steps) for source in range(first, last)])


def level_total(vector):
    return lax.psum(vector, ("tile", "sub"))


def seam_shift():
    sub_count = lax.axis_size("sub")
    return sub_count * TILE_ROW - sub_count + 1


def pad_block(current, flip_north, flip_south, first_sub, last_sub):
    block_width = current.shape[2]
    jump = seam_shift()
    west_col, east_col = [
        from_behind(strip, "tile", offset)
        for strip, offset in ((current[:, :, block_width - 1 :], 1), (current[:, :, :1], -1))
    ]
    extended = jnp.concatenate([west_col, current, east_col], axis=2)
    bottom_row = extended[:, ROWS - 1, :]
    top_row = extended[:, 0, :]
    inner_north, inner_south = [
        passed_along(strip, "sub", offset) for strip, offset in ((bottom_row, 1), (top_row, -1))
    ]
    seam_north, seam_south = [
        from_behind(strip, ("tile", "sub"), offset)
        for strip, offset in ((bottom_row, jump), (top_row, -jump))
    ]
    seam_north = jnp.where(flip_north, seam_north[:, ::-1], seam_north)
    north_row = jnp.where(first_sub, seam_north, inner_north)
    seam_south = jnp.where(flip_south, seam_south[:, ::-1], seam_south)
    south_row = jnp.where(last_sub, seam_south, inner_south)
    return jnp.concatenate([north_row[:, None], extended, south_row[:, None]], axis=1)


def unpad_block(pad_grad, flip_north, flip_south, first_sub, last_sub):
    block_width = pad_grad.shape[2] - 2
    jump = seam_shift()
    extended = pad_grad[:, 1:-1, :]
    north_grad = pad_grad[:, 0, :]
    south_grad = pad_grad[:, -1, :]
    unflip_north = jnp.where(flip_north, north_grad[:, ::-1], north_grad)
    unflip_south = jnp.where(flip_south, south_grad[:, ::-1], south_grad)
    nothing = jnp.zeros_like(north_grad)
    seam_bottom, seam_top = [
        from_behind(strip, ("tile", "sub"), offset)
        for strip, offset in (
            (jnp.where(first_sub, unflip_north, nothing), -jump),
            (jnp.where(last_sub, unflip_south, nothing), jump),
        )
    ]
    inner_bottom, inner_top = [
        passed_along(strip, "sub", offset)
        for strip, offset in (
            (jnp.where(first_sub, nothing, north_grad), -1),
            (jnp.where(last_sub, nothing, south_grad), 1),
        )
    ]
    extended = extended.at[:, ROWS - 1, :].add(seam_bottom + inner_bottom)
    extended = extended.at[:, 0, :].add(seam_top + inner_top)
    inner = extended[:, :, 1:-1]
    from_west, from_east = [
        from_behind(strip, "tile", offset)
        for strip, offset in ((extended[:, :, 0], -1), (extended[:, :, -1], 1))
    ]
    inner = inner.at[:, :, block_width - 1].add(from_west)
    inner = inner.at[:, :, 0].add(from_east)
    return inner


def gather_patches(padded, block_width):
    pieces = [
        padded[:, row_shift : row_shift + ROWS, col_shift : col_shift + block_width]
        for row_shift in range(3)
        for col_shift in range(3)
    ]
    return jnp.stack(pieces, axis=0).reshape(9 * LEVELS, ROWS * block_width)


def scatter_patches(patch_grad, block_width):
    pieces = patch_grad.reshape(9, LEVELS, ROWS, block_width)
    total = jnp.zeros((LEVELS, ROWS + 2, block_width + 2), jnp.float32)
    for row_shift in range(3):
        for col_shift in range(3):
            total = total + jnp.pad(
                pieces[3 * row_shift + col_shift],
                ((0, 0), (row_shift, 2 - row_shift), (col_shift, 2 - col_shift)),
            )
    return total


def shards(initial_state, cotangent, w_in, b_in, w_out, edge_flips):
    block_width = initial_state.shape[2] // ROWS
    total_cols = lax.axis_size("tile") * lax.axis_size("sub") * initial_state.shape[2]
    sub_index = lax.axis_index("sub")
    first_sub = sub_index == 0
    last_sub = sub_index == lax.axis_size("sub") - 1
    flip_north = edge_flips[0, 0] == 1
    flip_south = edge_flips[0, 1] == 1

    def network_input(current):
        padded = pad_block(
            current.astype(jnp.bfloat16), flip_north, flip_south, first_sub, last_sub
        )
        return gather_patches(padded, block_width)

    def first_layer(patch_vals):
        product = lax.dot_general(
            w_in, patch_vals, (((0,), (0,)), ((), ())), preferred_element_type=jnp.float32
        )
        return product + b_in[:, None]

    current = initial_state[0].reshape(LEVELS, ROWS, block_width)
    saved_fields = []
    for step_index in range(STEPS):
        saved_fields.append(current)
        patch_vals = network_input(current)
        pre_act = first_layer(patch_vals)
        hidden_vals = jax.nn.silu(pre_act).astype(jnp.bfloat16)
        tendency = jnp.dot(w_out, hidden_vals, preferred_element_type=jnp.float32)
        level_mean = level_total(jnp.sum(tendency, axis=1)) / total_cols
        current = current + (STEP_SIZE * (tendency - level_mean[:, None])).reshape(current.shape)
    gradient = cotangent[0]
    grad_w_in = jnp.zeros((w_in.shape[0], w_in.shape[1]), jnp.float32)
    grad_w_out = jnp.zeros((w_out.shape[0], w_out.shape[1]), jnp.float32)
    grad_b_in = jnp.zeros((w_in.shape[1],), jnp.float32)
    for step_index in reversed(range(STEPS)):
        scaled = STEP_SIZE * gradient
        level_grad = level_total(jnp.sum(scaled, axis=1)) / total_cols
        tend_grad = (scaled - level_grad[:, None]).astype(jnp.bfloat16)
        patch_vals = network_input(saved_fields[step_index])
        pre_act = first_layer(patch_vals)
        hidden_vals = jax.nn.silu(pre_act).astype(jnp.bfloat16)
        grad_w_out = grad_w_out + lax.dot_general(
            tend_grad, hidden_vals, (((1,), (1,)), ((), ())), preferred_element_type=jnp.float32
        )
        hidden_grad = lax.dot_general(
            w_out, tend_grad, (((0,), (0,)), ((), ())), preferred_element_type=jnp.float32
        )
        sigmoid_vals = jax.nn.sigmoid(pre_act)
        pre_grad = hidden_grad * sigmoid_vals * (1.0 + pre_act * (1.0 - sigmoid_vals))
        grad_b_in = grad_b_in + jnp.sum(pre_grad, axis=1)
        pre_low = pre_grad.astype(jnp.bfloat16)
        grad_w_in = grad_w_in + lax.dot_general(
            patch_vals, pre_low, (((1,), (1,)), ((), ())), preferred_element_type=jnp.float32
        )
        patch_grad = jnp.dot(w_in, pre_low, preferred_element_type=jnp.float32)
        pad_grad = scatter_patches(patch_grad, block_width)
        back_grad = unpad_block(pad_grad, flip_north, flip_south, first_sub, last_sub)
        gradient = gradient + back_grad.reshape(LEVELS, ROWS * block_width)
    quarters = (
        lax.psum_scatter(grad_w_in, "sub", scatter_dimension=1, tiled=True),
        lax.psum_scatter(grad_w_out, "sub", scatter_dimension=1, tiled=True),
        lax.psum_scatter(grad_b_in[None, :], "sub", scatter_dimension=1, tiled=True),
    )
    quarters = lax.psum((quarters[0], quarters[1], quarters[2]), "tile")
    grad_w_in, grad_w_out, bias_row = (
        lax.all_gather(quarters[0].astype(jnp.bfloat16), "sub", axis=1, tiled=True).astype(
            jnp.float32
        ),
        lax.all_gather(quarters[1].astype(jnp.bfloat16), "sub", axis=1, tiled=True).astype(
            jnp.float32
        ),
        lax.all_gather(quarters[2].astype(jnp.bfloat16), "sub", axis=1, tiled=True).astype(
            jnp.float32
        ),
    )
    grad_b_in = bias_row[0]
    final_block = current.reshape(1, LEVELS, ROWS * block_width)
    return (final_block, gradient[None], grad_w_in, grad_b_in, grad_w_out)


def solution(mesh):
    in_specs = (P("tile", None, "sub"), P("tile", None, "sub"), P(), P(), P(), P("tile", None))
    out_specs = (P("tile", None, "sub"), P("tile", None, "sub"), P(), P(), P())
    return jax.shard_map(shards, mesh=mesh, in_specs=in_specs, out_specs=out_specs, check_vma=False)
```

profile of v0, /device:TPU:0, one launch (start us, length us, event | category | flops | bytes accessed | tf_op | source)
XLA Modules:
  0.0 664.1 jit_solution(16025712312118512564)
XLA Ops:
  8.3 3.0 collective-permute-start
  11.3 3.1 collective-permute-start.1
  17.3 3.3 collective-permute-start.4
  23.2 2.2 collective-permute-start.3
  26.8 3.6 collective-permute-done.2
  33.8 40.8 %psum.77 = f32[64]{0:T(128)S(1)} all-reduce(f32[64]{0:T(128)S(1)} %get-tuple-element.323), channel_id=1, replica_groups=mesh['tile'=8,'sub'=4] {'tile','sub'}, use_global_device_ids=true, to_apply=%region_1.2 | all-reduce | flops 64 | bytes 512 | tf_op jit(solution)/shard_map/psum | solution.py:25
  75.3 2.3 collective-permute-start.6
  77.7 2.4 collective-permute-start.7
  83.1 4.1 collective-permute-start.9
  87.2 3.2 collective-permute-start.8
  90.5 1.6 collective-permute-done.8
  96.3 42.1 %psum.78 = f32[64]{0:T(128)S(1)} all-reduce(f32[64]{0:T(128)S(1)} %get-tuple-element.327), channel_id=1, replica_groups=mesh['tile'=8,'sub'=4] {'tile','sub'}, use_global_device_ids=true, to_apply=%region_3.4 | all-reduce | flops 64 | bytes 512 | tf_op jit(solution)/shard_map/psum | solution.py:25
  139.0 2.3 collective-permute-start.12
  141.3 2.4 collective-permute-start.13
  146.7 1.7 collective-permute-start.16
  150.0 3.6 collective-permute-start.14
  158.4 43.7 %all-reduce.37 = (f32[64]{0:T(128)S(1)}, f32[64]{0:T(128)S(1)}) all-reduce(f32[64]{0:T(128)S(1)} %get-tuple-element.331, f32[64]{0:T(128)S(1)} %fusion.26), channel_id=1, replica_groups=mesh['tile'=8,'sub'=4] {'tile','sub'}, use_global_device_ids=true, to_apply=%region_5.6 | all-reduce | flops 128 | bytes 1024 | tf_op jit(solution)/shard_map/psum | solution.py:25
  202.3 2.3 collective-permute-start.18
  204.6 2.4 collective-permute-start.19
  210.0 3.8 collective-permute-start.21
  213.9 3.7 collective-permute-start.20
  248.1 2.1 fusion.45
  250.2 3.2 collective-permute-start.27
  253.3 3.6 collective-permute-start.26
  257.0 2.3 collective-permute-done.26
  259.3 4.2 collective-permute-start.28
  265.3 6.3 collective-permute-done.29
  272.3 36.8 %psum.82 = f32[64]{0:T(128)S(1)} all-reduce(f32[64]{0:T(128)S(1)} %get-tuple-element.214), channel_id=1, replica_groups=mesh['tile'=8,'sub'=4] {'tile','sub'}, use_global_device_ids=true, to_apply=%region_11.12 | all-reduce | flops 64 | bytes 512 | tf_op jit(solution)/shard_map/psum | solution.py:25
  309.1 1.9 fusion.78
  323.5 1.6 copy.210
  325.1 1.6 copy.209
  333.0 2.9 collective-permute-start.30
  337.3 3.0 fusion.17
  340.3 4.5 collective-permute-start.33
  345.7 4.2 collective-permute-done.32
  350.5 1.6 scatter-add.61
  352.8 1.6 collective-permute-start.34
  354.4 1.7 copy_add_fusion.1
  358.9 4.5 collective-permute-done.35
  365.8 36.9 %psum.83 = f32[64]{0:T(128)} all-reduce(f32[64]{0:T(128)S(1)} %multiply_reduce_fusion.1), channel_id=1, replica_groups=mesh['tile'=8,'sub'=4] {'tile','sub'}, use_global_device_ids=true, to_apply=%region_13.14 | all-reduce | flops 64 | bytes 512 | tf_op jit(solution)/shard_map/psum | solution.py:25
  404.4 2.4 fusion.76
  408.2 1.6 copy.224
  413.0 1.6 copy.230
  428.9 2.9 collective-permute-start.36
  434.5 4.4 collective-permute-start.39
  439.7 4.2 collective-permute-done.38
  444.6 1.9 collective-permute-start.40
  449.6 5.1 collective-permute-done.41
  458.0 37.1 %all-reduce.36 = (f32[64]{0:T(128)}, f32[64]{0:T(128)}) all-reduce(f32[64]{0:T(128)} %get-tuple-element.335, f32[64]{0:T(128)S(1)} %multiply_reduce_fusion), channel_id=1, replica_groups=mesh['tile'=8,'sub'=4] {'tile','sub'}, use_global_device_ids=true, to_apply=%region_7.8 | all-reduce | flops 128 | bytes 1024 | tf_op jit(solution)/shard_map/psum | solution.py:25
  496.8 2.6 fusion.75
  500.6 2.1 convolution_add_fusion.4
  502.7 1.8 fusion.14
  504.8 2.0 add_add_fusion
  509.7 2.8 collective-permute-start.42
  513.7 9.6 %reduce-scatter.10.cloned.1.call-done = f32[256,1]{1,0:T(8,128)} async-done(((f32[1024,1]{1,0:T(8,128)}), f32[256,1]{1,0:T(8,128)}) %reduce-scatter.10.cloned.1.call-update) | async-done | bytes 1040
  524.3 21.9 %reduce-scatter.8.cloned.1.call-done = f32[64,256]{1,0:T(8,128)} async-done(((f32[64,1024]{1,0:T(8,128)}), f32[64,256]{1,0:T(8,128)}) %reduce-scatter.8.cloned.1.call-update) | async-done | bytes 65552 | tf_op jit(solution)/shard_map/reduce_scatter | solution.py:174
  546.2 35.9 %reduce-scatter.6.cloned.1.call-done = f32[576,256]{1,0:T(8,128)} async-done(((f32[576,1024]{1,0:T(8,128)}), f32[576,256]{1,0:T(8,128)}) %reduce-scatter.6.cloned.1.call-update) | async-done | bytes 589840 | tf_op jit(solution)/shard_map/reduce_scatter | solution.py:173
  582.1 44.4 %all-reduce.40 = (bf16[576,256]{1,0:T(8,128)(2,1)}, bf16[1,256]{1,0:T(2,128)(2,1)S(1)}, bf16[64,256]{1,0:T(8,128)(2,1)S(1)}) all-reduce(f32[576,256]{1,0:T(8,128)} %reduce-scatter.6.cloned.1.call-done, f32[1,256]{1,0:T(1,128)S(1)} %copy.248, f32[64,256]{1,0:T(8,128)} %reduce-scatter.8.cloned.1.call-done), channel_id=1, replica_groups=mesh['tile'=8,'sub'=4] {'tile'}, use_global_device_ids=true, to_apply=%region_17.18 | all-reduce | flops 164096 | bytes 984576 | tf_op jit(solution)/shard_map/psum | solution.py:177
  628.7 4.2 collective-permute-done.44
  632.9 1.9 collective-permute-start.46
  636.6 5.3 collective-permute-done.47
  642.8 5.1 all_gather.10
  648.5 5.4 all_gather.11
  654.6 3.0 convert_element_type.174
  (397 shorter events, 135.9 us)
Async XLA Ops:
  7.2 516.1 %reduce-scatter.10.cloned.1.call-start = ((), (), s32[]{:S(2)}) async-start(), calls=%async_computation.6 | async-start | bytes 655360
  8.3 7.6 %collective-permute-start = (bf16[64,8,1]{0,2,1:T(2,128)(2,1)S(1)}, bf16[64,8,1]{0,2,1:T(2,128)(2,1)S(1)}, u32[]{:S(2)}, u32[]{:S(2)}) collective-permute-start(bf16[64,8,1]{0,2,1:T(2,128)(2,1)S(1)} %get-tuple-element.317), channel_id=1, source_target_pairs={{0,4},{4,8},{8,12},{12,16},{16,20},{20,24},{24,28},{28,0},{1,5},{5... | collective-permute-start | bytes 3080 | tf_op jit(solution)/shard_map/ppermute | solution.py:15
  11.3 4.6 collective-permute-start.1
  16.0 10.8 %collective-permute-start.5 = (bf16[64,34]{0,1:T(8,128)(2,1)S(1)}, bf16[64,34]{0,1:T(8,128)(2,1)S(1)}, u32[]{:S(2)}, u32[]{:S(2)}) collective-permute-start(bf16[64,34]{0,1:T(8,128)(2,1)S(1)} %get-tuple-element.309), channel_id=1, source_target_pairs={{1,0},{2,1},{3,2},{5,4},{6,5},{7,6},{9,8},{10,9},{11,10},{13,12},{... | collective-permute-start | bytes 13064 | tf_op jit(solution)/shard_map/ppermute | solution.py:21
  17.3 9.5 %collective-permute-start.4 = (bf16[64,34]{0,1:T(8,128)(2,1)S(1)}, bf16[64,34]{0,1:T(8,128)(2,1)S(1)}, u32[]{:S(2)}, u32[]{:S(2)}) collective-permute-start(bf16[64,34]{0,1:T(8,128)(2,1)S(1)} %get-tuple-element.309), channel_id=1, source_target_pairs={{0,19},{1,20},{2,21},{3,22},{4,23},{5,24},{6,25},{7,26},{8,27},{9,... | collective-permute-start | bytes 13064 | tf_op jit(solution)/shard_map/ppermute | solution.py:15
  23.2 7.2 %collective-permute-start.3 = (bf16[64,34]{0,1:T(8,128)(2,1)S(1)}, bf16[64,34]{0,1:T(8,128)(2,1)S(1)}, u32[]{:S(2)}, u32[]{:S(2)}) collective-permute-start(bf16[64,34]{0,1:T(8,128)(2,1)S(1)} %get-tuple-element.310), channel_id=1, source_target_pairs={{0,1},{1,2},{2,3},{4,5},{5,6},{6,7},{8,9},{9,10},{10,11},{12,13},{... | collective-permute-start | bytes 13064 | tf_op jit(solution)/shard_map/ppermute | solution.py:21
  25.4 4.9 collective-permute-start.2
  75.3 6.4 collective-permute-start.6
  77.7 4.0 collective-permute-start.7
  81.7 8.7 %collective-permute-start.10 = (bf16[64,34]{0,1:T(8,128)(2,1)S(1)}, bf16[64,34]{0,1:T(8,128)(2,1)S(1)}, u32[]{:S(2)}, u32[]{:S(2)}) collective-permute-start(bf16[64,34]{0,1:T(8,128)(2,1)S(1)} %get-tuple-element.305), channel_id=1, source_target_pairs={{0,19},{1,20},{2,21},{3,22},{4,23},{5,24},{6,25},{7,26},{8,27},{9,... | collective-permute-start | bytes 13064 | tf_op jit(solution)/shard_map/ppermute | solution.py:15
  81.8 8.7 %collective-permute-start.11 = (bf16[64,34]{0,1:T(8,128)(2,1)S(1)}, bf16[64,34]{0,1:T(8,128)(2,1)S(1)}, u32[]{:S(2)}, u32[]{:S(2)}) collective-permute-start(bf16[64,34]{0,1:T(8,128)(2,1)S(1)} %get-tuple-element.305), channel_id=1, source_target_pairs={{1,0},{2,1},{3,2},{5,4},{6,5},{7,6},{9,8},{10,9},{11,10},{13,12},{... | collective-permute-start | bytes 13064 | tf_op jit(solution)/shard_map/ppermute | solution.py:21
  83.1 9.1 %collective-permute-start.9 = (bf16[64,34]{0,1:T(8,128)(2,1)S(1)}, bf16[64,34]{0,1:T(8,128)(2,1)S(1)}, u32[]{:S(2)}, u32[]{:S(2)}) collective-permute-start(bf16[64,34]{0,1:T(8,128)(2,1)S(1)} %get-tuple-element.306), channel_id=1, source_target_pairs={{0,1},{1,2},{2,3},{4,5},{5,6},{6,7},{8,9},{9,10},{10,11},{12,13},{... | collective-permute-start | bytes 13064 | tf_op jit(solution)/shard_map/ppermute | solution.py:21
  87.2 4.9 collective-permute-start.8
  139.0 6.4 collective-permute-start.12
  141.3 4.0 collective-permute-start.13
  145.4 8.2 %collective-permute-start.17 = (bf16[64,34]{0,1:T(8,128)(2,1)S(1)}, bf16[64,34]{0,1:T(8,128)(2,1)S(1)}, u32[]{:S(2)}, u32[]{:S(2)}) collective-permute-start(bf16[64,34]{0,1:T(8,128)(2,1)S(1)} %get-tuple-element.301), channel_id=1, source_target_pairs={{1,0},{2,1},{3,2},{5,4},{6,5},{7,6},{9,8},{10,9},{11,10},{13,12},{... | collective-permute-start | bytes 13064 | tf_op jit(solution)/shard_map/ppermute | solution.py:21
  146.7 6.9 %collective-permute-start.16 = (bf16[64,34]{0,1:T(8,128)(2,1)S(1)}, bf16[64,34]{0,1:T(8,128)(2,1)S(1)}, u32[]{:S(2)}, u32[]{:S(2)}) collective-permute-start(bf16[64,34]{0,1:T(8,128)(2,1)S(1)} %get-tuple-element.301), channel_id=1, source_target_pairs={{0,19},{1,20},{2,21},{3,22},{4,23},{5,24},{6,25},{7,26},{8,27},{9,... | collective-permute-start | bytes 13064 | tf_op jit(solution)/shard_map/ppermute | solution.py:15
  148.5 6.5 collective-permute-start.15
  150.0 5.0 collective-permute-start.14
  202.3 6.4 collective-permute-start.18
  204.6 4.0 collective-permute-start.19
  208.7 8.9 %collective-permute-start.22 = (bf16[64,34]{0,1:T(8,128)(2,1)S(1)}, bf16[64,34]{0,1:T(8,128)(2,1)S(1)}, u32[]{:S(2)}, u32[]{:S(2)}) collective-permute-start(bf16[64,34]{0,1:T(8,128)(2,1)S(1)} %get-tuple-element.297), channel_id=1, source_target_pairs={{0,19},{1,20},{2,21},{3,22},{4,23},{5,24},{6,25},{7,26},{8,27},{9,... | collective-permute-start | bytes 13064 | tf_op jit(solution)/shard_map/ppermute | solution.py:15
  208.7 8.9 %collective-permute-start.23 = (bf16[64,34]{0,1:T(8,128)(2,1)S(1)}, bf16[64,34]{0,1:T(8,128)(2,1)S(1)}, u32[]{:S(2)}, u32[]{:S(2)}) collective-permute-start(bf16[64,34]{0,1:T(8,128)(2,1)S(1)} %get-tuple-element.297), channel_id=1, source_target_pairs={{1,0},{2,1},{3,2},{5,4},{6,5},{7,6},{9,8},{10,9},{11,10},{13,12},{... | collective-permute-start | bytes 13064 | tf_op jit(solution)/shard_map/ppermute | solution.py:21
  210.0 9.0 %collective-permute-start.21 = (bf16[64,34]{0,1:T(8,128)(2,1)S(1)}, bf16[64,34]{0,1:T(8,128)(2,1)S(1)}, u32[]{:S(2)}, u32[]{:S(2)}) collective-permute-start(bf16[64,34]{0,1:T(8,128)(2,1)S(1)} %get-tuple-element.298), channel_id=1, source_target_pairs={{0,1},{1,2},{2,3},{4,5},{5,6},{6,7},{8,9},{9,10},{10,11},{12,13},{... | collective-permute-start | bytes 13064 | tf_op jit(solution)/shard_map/ppermute | solution.py:21
  213.9 5.1 collective-permute-start.20
  245.4 11.6 %collective-permute-start.24 = (f32[64,34]{0,1:T(8,128)S(1)}, f32[64,34]{0,1:T(8,128)S(1)}, u32[]{:S(2)}, u32[]{:S(2)}) collective-permute-start(f32[64,34]{0,1:T(8,128)S(1)} %get-tuple-element.279), channel_id=1, source_target_pairs={{0,19},{1,20},{2,21},{3,22},{4,23},{5,24},{6,25},{7,26},{8,27},{9,... | collective-permute-start | bytes 26120 | tf_op jit(solution)/shard_map/ppermute | solution.py:15
  246.8 10.1 %collective-permute-start.25 = (f32[64,34]{0,1:T(8,128)S(1)}, f32[64,34]{0,1:T(8,128)S(1)}, u32[]{:S(2)}, u32[]{:S(2)}) collective-permute-start(f32[64,34]{0,1:T(8,128)S(1)} %get-tuple-element.280), channel_id=1, source_target_pairs={{1,0},{2,1},{3,2},{5,4},{6,5},{7,6},{9,8},{10,9},{11,10},{13,12},{... | collective-permute-start | bytes 26120 | tf_op jit(solution)/shard_map/ppermute | solution.py:21
  250.2 6.8 %collective-permute-start.27 = (f32[64,34]{0,1:T(8,128)S(1)}, f32[64,34]{0,1:T(8,128)S(1)}, u32[]{:S(2)}, u32[]{:S(2)}) collective-permute-start(f32[64,34]{0,1:T(8,128)S(1)} %get-tuple-element.278), channel_id=1, source_target_pairs={{0,1},{1,2},{2,3},{4,5},{5,6},{6,7},{8,9},{9,10},{10,11},{12,13},{... | collective-permute-start | bytes 26120 | tf_op jit(solution)/shard_map/ppermute | solution.py:21
  253.3 6.0 collective-permute-start.26
  259.3 5.9 collective-permute-start.28
  265.2 6.4 collective-permute-start.29
  333.0 12.0 %collective-permute-start.30 = (f32[64,34]{0,1:T(8,128)S(1)}, f32[64,34]{0,1:T(8,128)S(1)}, u32[]{:S(2)}, u32[]{:S(2)}) collective-permute-start(f32[64,34]{0,1:T(8,128)S(1)} %get-tuple-element.273), channel_id=1, source_target_pairs={{0,19},{1,20},{2,21},{3,22},{4,23},{5,24},{6,25},{7,26},{8,27},{9,... | collective-permute-start | bytes 26120 | tf_op jit(solution)/shard_map/ppermute | solution.py:15
  335.8 9.1 %collective-permute-start.31 = (f32[64,34]{0,1:T(8,128)S(1)}, f32[64,34]{0,1:T(8,128)S(1)}, u32[]{:S(2)}, u32[]{:S(2)}) collective-permute-start(f32[64,34]{0,1:T(8,128)S(1)} %get-tuple-element.274), channel_id=1, source_target_pairs={{1,0},{2,1},{3,2},{5,4},{6,5},{7,6},{9,8},{10,9},{11,10},{13,12},{... | collective-permute-start | bytes 26120 | tf_op jit(solution)/shard_map/ppermute | solution.py:21
  340.3 5.4 collective-permute-start.33
  344.8 5.1 collective-permute-start.32
  352.8 4.7 collective-permute-start.34
  357.1 6.4 collective-permute-start.35
  428.9 10.7 %collective-permute-start.36 = (f32[64,34]{0,1:T(8,128)S(1)}, f32[64,34]{0,1:T(8,128)S(1)}, u32[]{:S(2)}, u32[]{:S(2)}) collective-permute-start(f32[64,34]{0,1:T(8,128)S(1)} %get-tuple-element.267), channel_id=1, source_target_pairs={{0,19},{1,20},{2,21},{3,22},{4,23},{5,24},{6,25},{7,26},{8,27},{9,... | collective-permute-start | bytes 26120 | tf_op jit(solution)/shard_map/ppermute | solution.py:15
  431.8 7.8 %collective-permute-start.37 = (f32[64,34]{0,1:T(8,128)S(1)}, f32[64,34]{0,1:T(8,128)S(1)}, u32[]{:S(2)}, u32[]{:S(2)}) collective-permute-start(f32[64,34]{0,1:T(8,128)S(1)} %get-tuple-element.268), channel_id=1, source_target_pairs={{1,0},{2,1},{3,2},{5,4},{6,5},{7,6},{9,8},{10,9},{11,10},{13,12},{... | collective-permute-start | bytes 26120 | tf_op jit(solution)/shard_map/ppermute | solution.py:21
  434.5 5.2 collective-permute-start.39
  438.9 5.1 collective-permute-start.38
  444.6 3.6 collective-permute-start.40
  448.1 6.6 collective-permute-start.41
  500.5 45.7 %reduce-scatter.8.cloned.1.call-start = ((), (), s32[]{:S(2)}) async-start(), calls=%async_computation.5 | async-start | bytes 327680 | tf_op jit(solution)/shard_map/reduce_scatter | solution.py:174
  502.7 79.4 %reduce-scatter.6.cloned.1.call-start = ((), (), s32[]{:S(2)}) async-start(), calls=%async_computation.3 | async-start | bytes 2949120 | tf_op jit(solution)/shard_map/reduce_scatter | solution.py:173
  506.8 147.8 %all-gather.2.cloned.1.call-start = ((), (), s32[]{:S(2)}) async-start(), calls=%async_computation.4 | async-start | bytes 1474560 | tf_op jit(solution)/shard_map/all_gather | solution.py:179
  509.3 117.2 %copy-start.53 = (f32[64]{0:T(128)S(1)}, f32[64]{0:T(128)}, u32[]{:S(2)}) copy-start(f32[64]{0:T(128)} %get-tuple-element.207) | copy-start | bytes 772
  509.5 125.3 %copy-start.34 = (f32[256,64]{0,1:T(8,128)S(1)}, f32[256,64]{0,1:T(8,128)}, u32[]{:S(2)}) copy-start(f32[256,64]{0,1:T(8,128)} %copy-done.33) | copy-start | bytes 196612
  509.5 125.3 %copy-start.36 = (f32[256,64]{0,1:T(8,128)S(1)}, f32[256,64]{0,1:T(8,128)}, u32[]{:S(2)}) copy-start(f32[256,64]{0,1:T(8,128)} %copy-done.35) | copy-start | bytes 196612
  509.5 125.3 %copy-start.38 = (f32[256,64]{0,1:T(8,128)S(1)}, f32[256,64]{0,1:T(8,128)}, u32[]{:S(2)}) copy-start(f32[256,64]{0,1:T(8,128)} %copy-done.37) | copy-start | bytes 196612
  509.5 125.3 %copy-start.41 = (f32[1,64,256]{2,1,0:T(8,128)S(1)}, f32[1,64,256]{2,1,0:T(8,128)}, u32[]{:S(2)}) copy-start(f32[1,64,256]{2,1,0:T(8,128)} %param.38) | copy-start | bytes 196612
  509.5 125.3 %copy-start.42 = (f32[256,64]{0,1:T(8,128)S(1)}, f32[256,64]{0,1:T(8,128)}, u32[]{:S(2)}) copy-start(f32[256,64]{0,1:T(8,128)} %get-tuple-element.336) | copy-start | bytes 196612
  509.5 125.3 %copy-start.47 = (f32[64]{0:T(128)S(1)}, f32[64]{0:T(128)}, u32[]{:S(2)}) copy-start(f32[64]{0:T(128)} %copy-done.46) | copy-start | bytes 772
  509.6 125.3 %copy-start.49 = (f32[64]{0:T(128)S(1)}, f32[64]{0:T(128)}, u32[]{:S(2)}) copy-start(f32[64]{0:T(128)} %copy-done.48) | copy-start | bytes 772
  509.6 132.4 %copy-start.4 = (f32[1,64,256]{1,2,0:T(8,128)S(1)}, f32[1,64,256]{1,2,0:T(8,128)}, u32[]{:S(2)}) copy-start(f32[1,64,256]{1,2,0:T(8,128)} %copy-done.2) | copy-start | bytes 196612
  509.6 132.4 %copy-start.5 = (f32[64,8,32]{0,2,1:T(8,128)S(1)}, f32[64,8,32]{0,2,1:T(8,128)}, u32[]{:S(2)}) copy-start(f32[64,8,32]{0,2,1:T(8,128)} %scatter-add.65) | copy-start | bytes 196612
  509.7 132.4 %copy-start.6 = (f32[64,8,32]{0,2,1:T(8,128)S(1)}, f32[64,8,32]{0,2,1:T(8,128)}, u32[]{:S(2)}) copy-start(f32[64,8,32]{0,2,1:T(8,128)} %scatter-add.71) | copy-start | bytes 196612
  509.7 132.4 %copy-start.26 = (f32[64,8,32]{0,2,1:T(8,128)S(1)}, f32[64,8,32]{0,2,1:T(8,128)}, u32[]{:S(2)}) copy-start(f32[64,8,32]{0,2,1:T(8,128)} %copy-done.25) | copy-start | bytes 196612
  509.7 118.3 %collective-permute-start.42 = (f32[64,34]{0,1:T(8,128)S(1)}, f32[64,34]{0,1:T(8,128)S(1)}, u32[]{:S(2)}, u32[]{:S(2)}) collective-permute-start(f32[64,34]{0,1:T(8,128)S(1)} %get-tuple-element.261), channel_id=1, source_target_pairs={{0,19},{1,20},{2,21},{3,22},{4,23},{5,24},{6,25},{7,26},{8,27},{9,... | collective-permute-start | bytes 26120 | tf_op jit(solution)/shard_map/ppermute | solution.py:15
  512.4 115.5 %collective-permute-start.43 = (f32[64,34]{0,1:T(8,128)S(1)}, f32[64,34]{0,1:T(8,128)S(1)}, u32[]{:S(2)}, u32[]{:S(2)}) collective-permute-start(f32[64,34]{0,1:T(8,128)S(1)} %get-tuple-element.262), channel_id=1, source_target_pairs={{1,0},{2,1},{3,2},{5,4},{6,5},{7,6},{9,8},{10,9},{11,10},{13,12},{... | collective-permute-start | bytes 26120 | tf_op jit(solution)/shard_map/ppermute | solution.py:21
  626.6 2.1 collective-permute-start.45
  627.9 5.1 collective-permute-start.44
  632.9 3.7 collective-permute-start.46
  635.6 6.4 collective-permute-start.47
  (45 other events, 614.7 us)
Sparse Core Ops, SparseCore 0:
  500.6 22.5 reduce-scatter.9
  526.3 19.8 reduce-scatter.7
  549.3 32.7 reduce-scatter.5
  626.6 15.1 all-gather.1
where the time goes:
time: 668 us; the launch traced here: 664 us
  blocking collectives  292 us (44%)
  waiting for transfers between devices  119 us (18%)
  starting transfers between devices  98 us (15%)
  local copies, waits for them, and re-layouts  82.4 us (12%)
  matrix products  32.2 us (5%)
  other arithmetic  23.4 us (4%)
  between operations  16.5 us (2%)
    psum x6, blocking collectives, level_total(): return lax.psum(vector, ('tile', 'sub'))  237 us
    ppermute x32, starting transfers between devices, from_behind(): lax.ppermute(value, axis, [(i, (i + by) % peers) for i in range(peers)])  62.4 us
    ppermute x32, waiting for transfers between devices, from_behind(): lax.ppermute(value, axis, [(i, (i + by) % peers) for i in range(peers)])  51.1 us
    slice x40, local copies, waits for them, and re-layouts, scatter_patches(): pieces[3 * row_shift + col_shift]  46.4 us
    psum x1, blocking collectives, shards(): quarters = lax.psum((quarters[0], quarters[1], quarters[2]), 'tile')  44.4 us
    reduce_scatter x1, waiting for transfers between devices, shards(): lax.psum_scatter(grad_w_in, 'sub', scatter_dimension=1, tiled=True)  35.9 us
    ppermute x16, starting transfers between devices, passed_along(): lax.ppermute(value, axis, [(source, source + steps) for source in range(f...  35.4 us
    reduce_scatter x1, waiting for transfers between devices, shards(): lax.psum_scatter(grad_w_out, 'sub', scatter_dimension=1, tiled=True)  21.9 us
  transfers between devices with their start and end apart: 52, of which 22 were waited for; matrix products, arithmetic and copies ran while one was open for 4% of the time, Pallas kernels for 0%

commit v1 on v0

--- a/solution.py
+++ b/solution.py
@@ -22,7 +22,7 @@
 
 
 def level_total(vector):
-    return lax.psum(vector, ("tile", "sub"))
+    return lax.psum(lax.psum(vector, "sub"), "tile")
 
 
 def seam_shift():

time: 668 us -> 569 us (0.85)
  blocking collectives: 292 us -> 209 us
  waiting for transfers between devices: 119 us -> 104 us
    psum x7 -> x13, blocking collectives: 282 us -> 198 us  [level_total(): return lax.psum(lax.psum(vector, 'sub'), 'tile')]
    ppermute x32, waiting for transfers between devices: 51.1 us -> 41.6 us  [from_behind(): lax.ppermute(value, axis, [(i, (i + by) % peers) for i in range(peers)])]
  transfers between devices with their start and end apart: 52 -> 52, of which waited for: 22 -> 19; matrix products, arithmetic and copies ran while one was open for 4% -> 5% of each run, Pallas kernels for 0% -> 0%
where the time goes in v1:
time: 569 us; the launch traced here: 565 us
  blocking collectives  209 us (37%)
  waiting for transfers between devices  104 us (18%)
  starting transfers between devices  99.7 us (18%)
  local copies, waits for them, and re-layouts  81.3 us (14%)
  matrix products  32.1 us (6%)
  other arithmetic  22.8 us (4%)
  between operations  16.6 us (3%)
    psum x13, blocking collectives, level_total(): return lax.psum(lax.psum(vector, 'sub'), 'tile')  198 us
    ppermute x32, starting transfers between devices, from_behind(): lax.ppermute(value, axis, [(i, (i + by) % peers) for i in range(peers)])  65.4 us
    slice x40, local copies, waits for them, and re-layouts, scatter_patches(): pieces[3 * row_shift + col_shift]  46.4 us
    ppermute x32, waiting for transfers between devices, from_behind(): lax.ppermute(value, axis, [(i, (i + by) % peers) for i in range(peers)])  41.6 us
    reduce_scatter x1, waiting for transfers between devices, shards(): lax.psum_scatter(grad_w_in, 'sub', scatter_dimension=1, tiled=True)  36 us
    ppermute x16, starting transfers between devices, passed_along(): lax.ppermute(value, axis, [(source, source + steps) for source in range(f...  34.1 us
    reduce_scatter x1, waiting for transfers between devices, shards(): lax.psum_scatter(grad_w_out, 'sub', scatter_dimension=1, tiled=True)  22.1 us
  transfers between devices with their start and end apart: 52, of which 19 were waited for; matrix products, arithmetic and copies ran while one was open for 5% of the time, Pallas kernels for 0%

profile of v1, /device:TPU:0, one launch (start us, length us, event | category | flops | bytes accessed | tf_op | source)
XLA Modules:
  0.0 565.2 jit_solution(7875607571825594358)
XLA Ops:
  8.3 3.0 collective-permute-start
  11.3 3.1 collective-permute-start.1
  17.3 3.3 collective-permute-start.4
  23.2 2.2 collective-permute-start.3
  26.8 3.6 collective-permute-done.2
  33.8 7.9 %psum.133 = f32[64]{0:T(128)S(1)} all-reduce(f32[64]{0:T(128)S(1)} %get-tuple-element.326), channel_id=1, replica_groups=mesh['tile'=8,'sub'=4] {'sub'}, use_global_device_ids=true, to_apply=%region_1.2 | all-reduce | flops 64 | bytes 512 | tf_op jit(solution)/shard_map/psum | solution.py:25
  41.6 18.6 %psum.134 = f32[64]{0:T(128)S(1)} all-reduce(f32[64]{0:T(128)S(1)} %psum.133), channel_id=1, replica_groups=mesh['tile'=8,'sub'=4] {'tile'}, use_global_device_ids=true, to_apply=%region_2.3 | all-reduce | flops 64 | bytes 512 | tf_op jit(solution)/shard_map/psum | solution.py:25
  61.6 4.2 collective-permute-start.7
  68.8 3.0 collective-permute-start.9
  71.9 3.9 collective-permute-start.8
  80.6 6.5 %psum.135 = f32[64]{0:T(128)S(1)} all-reduce(f32[64]{0:T(128)S(1)} %get-tuple-element.330), channel_id=1, replica_groups=mesh['tile'=8,'sub'=4] {'sub'}, use_global_device_ids=true, to_apply=%region_4.5 | all-reduce | flops 64 | bytes 512 | tf_op jit(solution)/shard_map/psum | solution.py:25
  87.1 22.0 %psum.136 = f32[64]{0:T(128)S(1)} all-reduce(f32[64]{0:T(128)S(1)} %psum.135), channel_id=1, replica_groups=mesh['tile'=8,'sub'=4] {'tile'}, use_global_device_ids=true, to_apply=%region_5.6 | all-reduce | flops 64 | bytes 512 | tf_op jit(solution)/shard_map/psum | solution.py:25
  110.0 4.7 collective-permute-start.13
  117.7 3.0 collective-permute-start.15
  120.8 3.8 collective-permute-start.14
  129.3 5.9 %all-reduce.39 = (f32[64]{0:T(128)S(1)}, f32[64]{0:T(128)S(1)}) all-reduce(f32[64]{0:T(128)S(1)} %get-tuple-element.334, f32[64]{0:T(128)S(1)} %fusion.26), channel_id=1, replica_groups=mesh['tile'=8,'sub'=4] {'sub'}, use_global_device_ids=true, to_apply=%region_7.8 | all-reduce | flops 128 | bytes 1024 | tf_op jit(solution)/shard_map/psum | solution.py:25
  135.2 22.6 %all-reduce.37 = (f32[64]{0:T(128)S(1)}, f32[64]{0:T(128)S(1)}) all-reduce(f32[64]{0:T(128)S(1)} %get-tuple-element.215, f32[64]{0:T(128)S(1)} %get-tuple-element.216), channel_id=1, replica_groups=mesh['tile'=8,'sub'=4] {'tile'}, use_global_device_ids=true, to_apply=%region_8.9 | all-reduce | flops 128 | bytes 1024 | tf_op jit(solution)/shard_map/psum | solution.py:25
  158.1 4.7 collective-permute-start.19
  165.8 3.0 collective-permute-start.21
  168.8 4.1 collective-permute-start.20
  183.2 1.6 copy.200
  202.9 2.1 fusion.45
  204.9 3.2 collective-permute-start.27
  208.1 3.1 collective-permute-start.26
  211.2 3.3 collective-permute-done.26
  214.5 4.7 collective-permute-start.28
  221.0 6.3 %collective-permute-done.29 = f32[64,8]{0,1:T(8,128)S(1)} collective-permute-done((f32[64,8]{0,1:T(8,128)S(1)}, f32[64,8]{0,1:T(8,128)S(1)}, u32[]{:S(2)}, u32[]{:S(2)}) %collective-permute-start.29) | collective-permute-done | bytes 2080 | tf_op jit(solution)/shard_map/ppermute | solution.py:15
  228.0 5.7 %psum.143 = f32[64]{0:T(128)S(1)} all-reduce(f32[64]{0:T(128)S(1)} %get-tuple-element.217), channel_id=1, replica_groups=mesh['tile'=8,'sub'=4] {'sub'}, use_global_device_ids=true, to_apply=%region_16.17 | all-reduce | flops 64 | bytes 512 | tf_op jit(solution)/shard_map/psum | solution.py:25
  233.8 17.1 %psum.144 = f32[64]{0:T(128)S(1)} all-reduce(f32[64]{0:T(128)S(1)} %psum.143), channel_id=1, replica_groups=mesh['tile'=8,'sub'=4] {'tile'}, use_global_device_ids=true, to_apply=%region_17.18 | all-reduce | flops 64 | bytes 512 | tf_op jit(solution)/shard_map/psum | solution.py:25
  250.9 1.9 fusion.78
  254.2 1.6 copy.208
  276.2 3.0 fusion.17
  279.3 3.0 collective-permute-start.33
  282.3 3.9 collective-permute-start.32
  288.3 1.6 scatter-add.61
  290.7 2.9 collective-permute-start.34
  293.6 1.7 copy_add_fusion.1
  297.6 4.9 collective-permute-done.35
  305.0 6.4 %psum.145 = f32[64]{0:T(128)} all-reduce(f32[64]{0:T(128)S(1)} %multiply_reduce_fusion.1), channel_id=1, replica_groups=mesh['tile'=8,'sub'=4] {'sub'}, use_global_device_ids=true, to_apply=%region_19.20 | all-reduce | flops 64 | bytes 512 | tf_op jit(solution)/shard_map/psum | solution.py:25
  311.3 17.2 %psum.146 = f32[64]{0:T(128)S(1)} all-reduce(f32[64]{0:T(128)} %psum.145), channel_id=1, replica_groups=mesh['tile'=8,'sub'=4] {'tile'}, use_global_device_ids=true, to_apply=%region_20.21 | all-reduce | flops 64 | bytes 512 | tf_op jit(solution)/shard_map/psum | solution.py:25
  329.6 2.4 fusion.76
  336.6 1.6 copy.231
  341.4 1.6 copy.228
  356.8 3.0 collective-permute-start.39
  359.9 3.9 collective-permute-start.38
  366.0 2.8 collective-permute-start.40
  371.8 5.2 collective-permute-done.41
  380.3 6.5 %all-reduce.38 = (f32[64]{0:T(128)}, f32[64]{0:T(128)}) all-reduce(f32[64]{0:T(128)} %get-tuple-element.338, f32[64]{0:T(128)S(1)} %multiply_reduce_fusion), channel_id=1, replica_groups=mesh['tile'=8,'sub'=4] {'sub'}, use_global_device_ids=true, to_apply=%region_10.11 | all-reduce | flops 128 | bytes 1024 | tf_op jit(solution)/shard_map/psum | solution.py:25
  386.7 17.5 %psum.148 = f32[64]{0:T(128)S(1)} all-reduce(f32[64]{0:T(128)} %get-tuple-element.214), channel_id=1, replica_groups=mesh['tile'=8,'sub'=4] {'tile'}, use_global_device_ids=true, to_apply=%region_23.24 | all-reduce | flops 64 | bytes 512 | tf_op jit(solution)/shard_map/psum | solution.py:25
  405.3 2.6 fusion.75
  409.0 2.1 convolution_add_fusion.4
  411.2 1.8 fusion.14
  413.3 2.0 add_add_fusion
  419.6 3.0 collective-permute-start.45
  422.6 3.8 collective-permute-start.44
  426.4 4.0 reduce-scatter.10.cloned.1.call-done
  431.4 22.1 %reduce-scatter.8.cloned.1.call-done = f32[64,256]{1,0:T(8,128)} async-done(((f32[64,1024]{1,0:T(8,128)}), f32[64,256]{1,0:T(8,128)}) %reduce-scatter.8.cloned.1.call-update) | async-done | bytes 65552 | tf_op jit(solution)/shard_map/reduce_scatter | solution.py:174
  453.5 36.0 %reduce-scatter.6.cloned.1.call-done = f32[576,256]{1,0:T(8,128)} async-done(((f32[576,1024]{1,0:T(8,128)}), f32[576,256]{1,0:T(8,128)}) %reduce-scatter.6.cloned.1.call-update) | async-done | bytes 589840 | tf_op jit(solution)/shard_map/reduce_scatter | solution.py:173
  489.5 44.4 %all-reduce.41 = (f32[64]{0:T(128)S(1)}, bf16[576,256]{1,0:T(8,128)(2,1)}, bf16[1,256]{1,0:T(2,128)(2,1)S(1)}, bf16[64,256]{1,0:T(8,128)(2,1)S(1)}) all-reduce(f32[64]{0:T(128)S(1)} %copy-done.53, f32[576,256]{1,0:T(8,128)} %reduce-scatter.6.cloned.1.call-done, f32[1,256]{1,0:T(1,128)S(1)} %copy.248, ...), channel_id=1, replica_groups=mesh['tile'=8,'sub'=4] {'tile'}, use_global_device_ids=true, to_apply=%region_11.12 | all-reduce | flops 164160 | bytes 985088 | tf_op jit(solution)/shard_map/psum | solution.py:25
  534.0 1.8 collective-permute-start.46
  537.7 4.5 collective-permute-done.47
  543.0 5.2 all_gather.10
  548.8 5.4 all_gather.11
  555.7 3.0 convert_element_type.174
  (405 shorter events, 134.2 us)
Async XLA Ops:
  7.2 423.2 %reduce-scatter.10.cloned.1.call-start = ((), (), s32[]{:S(2)}) async-start(), calls=%async_computation.6 | async-start | bytes 655360
  8.3 7.6 %collective-permute-start = (bf16[64,8,1]{0,2,1:T(2,128)(2,1)S(1)}, bf16[64,8,1]{0,2,1:T(2,128)(2,1)S(1)}, u32[]{:S(2)}, u32[]{:S(2)}) collective-permute-start(bf16[64,8,1]{0,2,1:T(2,128)(2,1)S(1)} %get-tuple-element.320), channel_id=1, source_target_pairs={{0,4},{4,8},{8,12},{12,16},{16,20},{20,24},{24,28},{28,0},{1,5},{5... | collective-permute-start | bytes 3080 | tf_op jit(solution)/shard_map/ppermute | solution.py:15
  11.3 4.6 collective-permute-start.1
  16.0 10.8 %collective-permute-start.5 = (bf16[64,34]{0,1:T(8,128)(2,1)S(1)}, bf16[64,34]{0,1:T(8,128)(2,1)S(1)}, u32[]{:S(2)}, u32[]{:S(2)}) collective-permute-start(bf16[64,34]{0,1:T(8,128)(2,1)S(1)} %get-tuple-element.312), channel_id=1, source_target_pairs={{1,0},{2,1},{3,2},{5,4},{6,5},{7,6},{9,8},{10,9},{11,10},{13,12},{... | collective-permute-start | bytes 13064 | tf_op jit(solution)/shard_map/ppermute | solution.py:21
  17.3 9.5 %collective-permute-start.4 = (bf16[64,34]{0,1:T(8,128)(2,1)S(1)}, bf16[64,34]{0,1:T(8,128)(2,1)S(1)}, u32[]{:S(2)}, u32[]{:S(2)}) collective-permute-start(bf16[64,34]{0,1:T(8,128)(2,1)S(1)} %get-tuple-element.312), channel_id=1, source_target_pairs={{0,19},{1,20},{2,21},{3,22},{4,23},{5,24},{6,25},{7,26},{8,27},{9,... | collective-permute-start | bytes 13064 | tf_op jit(solution)/shard_map/ppermute | solution.py:15
  23.2 7.2 %collective-permute-start.3 = (bf16[64,34]{0,1:T(8,128)(2,1)S(1)}, bf16[64,34]{0,1:T(8,128)(2,1)S(1)}, u32[]{:S(2)}, u32[]{:S(2)}) collective-permute-start(bf16[64,34]{0,1:T(8,128)(2,1)S(1)} %get-tuple-element.313), channel_id=1, source_target_pairs={{0,1},{1,2},{2,3},{4,5},{5,6},{6,7},{8,9},{9,10},{10,11},{12,13},{... | collective-permute-start | bytes 13064 | tf_op jit(solution)/shard_map/ppermute | solution.py:21
  25.4 4.9 collective-permute-start.2
  33.4 44.0 %copy-start.9 = (bf16[1024,256]{0,1:T(8,128)(2,1)}, bf16[1024,256]{0,1:T(8,128)(2,1)S(1)}, u32[]{:S(2)}) copy-start(bf16[1024,256]{0,1:T(8,128)(2,1)S(1)} %get-tuple-element.324) | copy-start | bytes 1572868
  61.1 6.4 %collective-permute-start.6 = (bf16[64,8,1]{0,2,1:T(2,128)(2,1)S(1)}, bf16[64,8,1]{0,2,1:T(2,128)(2,1)S(1)}, u32[]{:S(2)}, u32[]{:S(2)}) collective-permute-start(bf16[64,8,1]{0,2,1:T(2,128)(2,1)S(1)} %get-tuple-element.318), channel_id=1, source_target_pairs={{0,4},{4,8},{8,12},{12,16},{16,20},{20,24},{24,28},{28,0},{1,5},{5... | collective-permute-start | bytes 3080 | tf_op jit(solution)/shard_map/ppermute | solution.py:15
  61.6 5.8 %collective-permute-start.7 = (bf16[64,8,1]{0,2,1:T(2,128)(2,1)S(1)}, bf16[64,8,1]{0,2,1:T(2,128)(2,1)S(1)}, u32[]{:S(2)}, u32[]{:S(2)}) collective-permute-start(bf16[64,8,1]{0,2,1:T(2,128)(2,1)S(1)} %get-tuple-element.319), channel_id=1, source_target_pairs={{0,28},{4,0},{8,4},{12,8},{16,12},{20,16},{24,20},{28,24},{1,29},{... | collective-permute-start | bytes 3080 | tf_op jit(solution)/shard_map/ppermute | solution.py:15
  67.5 8.3 %collective-permute-start.10 = (bf16[64,34]{0,1:T(8,128)(2,1)S(1)}, bf16[64,34]{0,1:T(8,128)(2,1)S(1)}, u32[]{:S(2)}, u32[]{:S(2)}) collective-permute-start(bf16[64,34]{0,1:T(8,128)(2,1)S(1)} %get-tuple-element.308), channel_id=1, source_target_pairs={{0,19},{1,20},{2,21},{3,22},{4,23},{5,24},{6,25},{7,26},{8,27},{9,... | collective-permute-start | bytes 13064 | tf_op jit(solution)/shard_map/ppermute | solution.py:15
  67.5 8.3 %collective-permute-start.11 = (bf16[64,34]{0,1:T(8,128)(2,1)S(1)}, bf16[64,34]{0,1:T(8,128)(2,1)S(1)}, u32[]{:S(2)}, u32[]{:S(2)}) collective-permute-start(bf16[64,34]{0,1:T(8,128)(2,1)S(1)} %get-tuple-element.308), channel_id=1, source_target_pairs={{1,0},{2,1},{3,2},{5,4},{6,5},{7,6},{9,8},{10,9},{11,10},{13,12},{... | collective-permute-start | bytes 13064 | tf_op jit(solution)/shard_map/ppermute | solution.py:21
  68.8 8.4 %collective-permute-start.9 = (bf16[64,34]{0,1:T(8,128)(2,1)S(1)}, bf16[64,34]{0,1:T(8,128)(2,1)S(1)}, u32[]{:S(2)}, u32[]{:S(2)}) collective-permute-start(bf16[64,34]{0,1:T(8,128)(2,1)S(1)} %get-tuple-element.309), channel_id=1, source_target_pairs={{0,1},{1,2},{2,3},{4,5},{5,6},{6,7},{8,9},{9,10},{10,11},{12,13},{... | collective-permute-start | bytes 13064 | tf_op jit(solution)/shard_map/ppermute | solution.py:21
  71.9 5.3 collective-permute-start.8
  80.2 45.9 %copy-start.10 = (bf16[1024,256]{0,1:T(8,128)(2,1)}, bf16[1024,256]{0,1:T(8,128)(2,1)S(1)}, u32[]{:S(2)}) copy-start(bf16[1024,256]{0,1:T(8,128)(2,1)S(1)} %get-tuple-element.328) | copy-start | bytes 1572868
  80.2 34.5 %copy-start.45 = (f32[1,64,256]{2,1,0:T(8,128)S(1)}, f32[1,64,256]{2,1,0:T(8,128)}, u32[]{:S(2)}) copy-start(f32[1,64,256]{2,1,0:T(8,128)} %param.39) | copy-start | bytes 196612
  109.9 6.4 %collective-permute-start.12 = (bf16[64,8,1]{0,2,1:T(2,128)(2,1)S(1)}, bf16[64,8,1]{0,2,1:T(2,128)(2,1)S(1)}, u32[]{:S(2)}, u32[]{:S(2)}) collective-permute-start(bf16[64,8,1]{0,2,1:T(2,128)(2,1)S(1)} %get-tuple-element.316), channel_id=1, source_target_pairs={{0,4},{4,8},{8,12},{12,16},{16,20},{20,24},{24,28},{28,0},{1,5},{5... | collective-permute-start | bytes 3080 | tf_op jit(solution)/shard_map/ppermute | solution.py:15
  110.0 6.3 %collective-permute-start.13 = (bf16[64,8,1]{0,2,1:T(2,128)(2,1)S(1)}, bf16[64,8,1]{0,2,1:T(2,128)(2,1)S(1)}, u32[]{:S(2)}, u32[]{:S(2)}) collective-permute-start(bf16[64,8,1]{0,2,1:T(2,128)(2,1)S(1)} %get-tuple-element.317), channel_id=1, source_target_pairs={{0,28},{4,0},{8,4},{12,8},{16,12},{20,16},{24,20},{28,24},{1,29},{... | collective-permute-start | bytes 3080 | tf_op jit(solution)/shard_map/ppermute | solution.py:15
  114.8 62.4 %copy-start.2 = (f32[1,64,256]{1,2,0:T(8,128)}, f32[1,64,256]{1,2,0:T(8,128)S(1)}, u32[]{:S(2)}) copy-start(f32[1,64,256]{1,2,0:T(8,128)S(1)} %copy.206) | copy-start | bytes 196612
  116.3 8.2 %collective-permute-start.17 = (bf16[64,34]{0,1:T(8,128)(2,1)S(1)}, bf16[64,34]{0,1:T(8,128)(2,1)S(1)}, u32[]{:S(2)}, u32[]{:S(2)}) collective-permute-start(bf16[64,34]{0,1:T(8,128)(2,1)S(1)} %get-tuple-element.304), channel_id=1, source_target_pairs={{1,0},{2,1},{3,2},{5,4},{6,5},{7,6},{9,8},{10,9},{11,10},{13,12},{... | collective-permute-start | bytes 13064 | tf_op jit(solution)/shard_map/ppermute | solution.py:21
  117.6 6.9 %collective-permute-start.16 = (bf16[64,34]{0,1:T(8,128)(2,1)S(1)}, bf16[64,34]{0,1:T(8,128)(2,1)S(1)}, u32[]{:S(2)}, u32[]{:S(2)}) collective-permute-start(bf16[64,34]{0,1:T(8,128)(2,1)S(1)} %get-tuple-element.304), channel_id=1, source_target_pairs={{0,19},{1,20},{2,21},{3,22},{4,23},{5,24},{6,25},{7,26},{8,27},{9,... | collective-permute-start | bytes 13064 | tf_op jit(solution)/shard_map/ppermute | solution.py:15
  117.7 8.2 %collective-permute-start.15 = (bf16[64,34]{0,1:T(8,128)(2,1)S(1)}, bf16[64,34]{0,1:T(8,128)(2,1)S(1)}, u32[]{:S(2)}, u32[]{:S(2)}) collective-permute-start(bf16[64,34]{0,1:T(8,128)(2,1)S(1)} %get-tuple-element.305), channel_id=1, source_target_pairs={{0,1},{1,2},{2,3},{4,5},{5,6},{6,7},{8,9},{9,10},{10,11},{12,13},{... | collective-permute-start | bytes 13064 | tf_op jit(solution)/shard_map/ppermute | solution.py:21
  120.8 5.1 collective-permute-start.14
  127.3 30.7 %copy-start.39 = (f32[64,8,32]{0,2,1:T(8,128)S(1)}, f32[64,8,32]{0,2,1:T(8,128)}, u32[]{:S(2)}) copy-start(f32[64,8,32]{0,2,1:T(8,128)} %get-tuple-element.222) | copy-start | bytes 196612
  128.9 45.7 %copy-start.12 = (bf16[1024,256]{0,1:T(8,128)(2,1)}, bf16[1024,256]{0,1:T(8,128)(2,1)S(1)}, u32[]{:S(2)}) copy-start(bf16[1024,256]{0,1:T(8,128)(2,1)S(1)} %get-tuple-element.332) | copy-start | bytes 1572868
  129.3 28.7 %copy-start.37 = (f32[256,64]{0,1:T(8,128)}, f32[256,64]{0,1:T(8,128)S(1)}, u32[]{:S(2)}) copy-start(f32[256,64]{0,1:T(8,128)S(1)} %get-tuple-element.335) | copy-start | bytes 196612
  158.0 6.4 %collective-permute-start.18 = (bf16[64,8,1]{0,2,1:T(2,128)(2,1)S(1)}, bf16[64,8,1]{0,2,1:T(2,128)(2,1)S(1)}, u32[]{:S(2)}, u32[]{:S(2)}) collective-permute-start(bf16[64,8,1]{0,2,1:T(2,128)(2,1)S(1)} %get-tuple-element.314), channel_id=1, source_target_pairs={{0,4},{4,8},{8,12},{12,16},{16,20},{20,24},{24,28},{28,0},{1,5},{5... | collective-permute-start | bytes 3080 | tf_op jit(solution)/shard_map/ppermute | solution.py:15
  158.1 6.3 %collective-permute-start.19 = (bf16[64,8,1]{0,2,1:T(2,128)(2,1)S(1)}, bf16[64,8,1]{0,2,1:T(2,128)(2,1)S(1)}, u32[]{:S(2)}, u32[]{:S(2)}) collective-permute-start(bf16[64,8,1]{0,2,1:T(2,128)(2,1)S(1)} %get-tuple-element.315), channel_id=1, source_target_pairs={{0,28},{4,0},{8,4},{12,8},{16,12},{20,16},{24,20},{28,24},{1,29},{... | collective-permute-start | bytes 3080 | tf_op jit(solution)/shard_map/ppermute | solution.py:15
  164.4 8.5 %collective-permute-start.22 = (bf16[64,34]{0,1:T(8,128)(2,1)S(1)}, bf16[64,34]{0,1:T(8,128)(2,1)S(1)}, u32[]{:S(2)}, u32[]{:S(2)}) collective-permute-start(bf16[64,34]{0,1:T(8,128)(2,1)S(1)} %get-tuple-element.300), channel_id=1, source_target_pairs={{0,19},{1,20},{2,21},{3,22},{4,23},{5,24},{6,25},{7,26},{8,27},{9,... | collective-permute-start | bytes 13064 | tf_op jit(solution)/shard_map/ppermute | solution.py:15
  164.5 8.5 %collective-permute-start.23 = (bf16[64,34]{0,1:T(8,128)(2,1)S(1)}, bf16[64,34]{0,1:T(8,128)(2,1)S(1)}, u32[]{:S(2)}, u32[]{:S(2)}) collective-permute-start(bf16[64,34]{0,1:T(8,128)(2,1)S(1)} %get-tuple-element.300), channel_id=1, source_target_pairs={{1,0},{2,1},{3,2},{5,4},{6,5},{7,6},{9,8},{10,9},{11,10},{13,12},{... | collective-permute-start | bytes 13064 | tf_op jit(solution)/shard_map/ppermute | solution.py:21
  165.8 8.6 %collective-permute-start.21 = (bf16[64,34]{0,1:T(8,128)(2,1)S(1)}, bf16[64,34]{0,1:T(8,128)(2,1)S(1)}, u32[]{:S(2)}, u32[]{:S(2)}) collective-permute-start(bf16[64,34]{0,1:T(8,128)(2,1)S(1)} %get-tuple-element.301), channel_id=1, source_target_pairs={{0,1},{1,2},{2,3},{4,5},{5,6},{6,7},{8,9},{9,10},{10,11},{12,13},{... | collective-permute-start | bytes 13064 | tf_op jit(solution)/shard_map/ppermute | solution.py:21
  168.8 5.5 collective-permute-start.20
  200.7 10.5 %collective-permute-start.24 = (f32[64,34]{0,1:T(8,128)S(1)}, f32[64,34]{0,1:T(8,128)S(1)}, u32[]{:S(2)}, u32[]{:S(2)}) collective-permute-start(f32[64,34]{0,1:T(8,128)S(1)} %get-tuple-element.282), channel_id=1, source_target_pairs={{0,19},{1,20},{2,21},{3,22},{4,23},{5,24},{6,25},{7,26},{8,27},{9,... | collective-permute-start | bytes 26120 | tf_op jit(solution)/shard_map/ppermute | solution.py:15
  201.6 9.6 %collective-permute-start.25 = (f32[64,34]{0,1:T(8,128)S(1)}, f32[64,34]{0,1:T(8,128)S(1)}, u32[]{:S(2)}, u32[]{:S(2)}) collective-permute-start(f32[64,34]{0,1:T(8,128)S(1)} %get-tuple-element.283), channel_id=1, source_target_pairs={{1,0},{2,1},{3,2},{5,4},{6,5},{7,6},{9,8},{10,9},{11,10},{13,12},{... | collective-permute-start | bytes 26120 | tf_op jit(solution)/shard_map/ppermute | solution.py:21
  204.9 6.3 %collective-permute-start.27 = (f32[64,34]{0,1:T(8,128)S(1)}, f32[64,34]{0,1:T(8,128)S(1)}, u32[]{:S(2)}, u32[]{:S(2)}) collective-permute-start(f32[64,34]{0,1:T(8,128)S(1)} %get-tuple-element.281), channel_id=1, source_target_pairs={{0,1},{1,2},{2,3},{4,5},{5,6},{6,7},{8,9},{9,10},{10,11},{12,13},{... | collective-permute-start | bytes 26120 | tf_op jit(solution)/shard_map/ppermute | solution.py:21
  208.1 6.4 %collective-permute-start.26 = (f32[64,34]{0,1:T(8,128)S(1)}, f32[64,34]{0,1:T(8,128)S(1)}, u32[]{:S(2)}, u32[]{:S(2)}) collective-permute-start(f32[64,34]{0,1:T(8,128)S(1)} %get-tuple-element.284), channel_id=1, source_target_pairs={{0,13},{1,14},{2,15},{3,16},{4,17},{5,18},{6,19},{7,20},{8,21},{9,... | collective-permute-start | bytes 26120 | tf_op jit(solution)/shard_map/ppermute | solution.py:15
  214.5 6.5 %collective-permute-start.28 = (f32[64,8]{0,1:T(8,128)S(1)}, f32[64,8]{0,1:T(8,128)S(1)}, u32[]{:S(2)}, u32[]{:S(2)}) collective-permute-start(f32[64,8]{0,1:T(8,128)S(1)} %bitcast.528), channel_id=1, source_target_pairs={{0,28},{4,0},{8,4},{12,8},{16,12},{20,16},{24,20},{28,24},{1,29},{... | collective-permute-start | bytes 6152 | tf_op jit(solution)/shard_map/ppermute | solution.py:15
  220.9 6.4 %collective-permute-start.29 = (f32[64,8]{0,1:T(8,128)S(1)}, f32[64,8]{0,1:T(8,128)S(1)}, u32[]{:S(2)}, u32[]{:S(2)}) collective-permute-start(f32[64,8]{0,1:T(8,128)S(1)} %bitcast.526), channel_id=1, source_target_pairs={{0,4},{4,8},{8,12},{12,16},{16,20},{20,24},{24,28},{28,0},{1,5},{5... | collective-permute-start | bytes 6152 | tf_op jit(solution)/shard_map/ppermute | solution.py:15
  274.7 11.5 %collective-permute-start.30 = (f32[64,34]{0,1:T(8,128)S(1)}, f32[64,34]{0,1:T(8,128)S(1)}, u32[]{:S(2)}, u32[]{:S(2)}) collective-permute-start(f32[64,34]{0,1:T(8,128)S(1)} %get-tuple-element.276), channel_id=1, source_target_pairs={{0,19},{1,20},{2,21},{3,22},{4,23},{5,24},{6,25},{7,26},{8,27},{9,... | collective-permute-start | bytes 26120 | tf_op jit(solution)/shard_map/ppermute | solution.py:15
  274.8 11.4 %collective-permute-start.31 = (f32[64,34]{0,1:T(8,128)S(1)}, f32[64,34]{0,1:T(8,128)S(1)}, u32[]{:S(2)}, u32[]{:S(2)}) collective-permute-start(f32[64,34]{0,1:T(8,128)S(1)} %get-tuple-element.277), channel_id=1, source_target_pairs={{1,0},{2,1},{3,2},{5,4},{6,5},{7,6},{9,8},{10,9},{11,10},{13,12},{... | collective-permute-start | bytes 26120 | tf_op jit(solution)/shard_map/ppermute | solution.py:21
  279.3 7.7 %collective-permute-start.33 = (f32[64,34]{0,1:T(8,128)S(1)}, f32[64,34]{0,1:T(8,128)S(1)}, u32[]{:S(2)}, u32[]{:S(2)}) collective-permute-start(f32[64,34]{0,1:T(8,128)S(1)} %get-tuple-element.275), channel_id=1, source_target_pairs={{0,1},{1,2},{2,3},{4,5},{5,6},{6,7},{8,9},{9,10},{10,11},{12,13},{... | collective-permute-start | bytes 26120 | tf_op jit(solution)/shard_map/ppermute | solution.py:21
  282.3 5.4 collective-permute-start.32
  290.7 5.6 collective-permute-start.34
  296.2 6.4 %collective-permute-start.35 = (f32[64,8]{0,1:T(8,128)S(1)}, f32[64,8]{0,1:T(8,128)S(1)}, u32[]{:S(2)}, u32[]{:S(2)}) collective-permute-start(f32[64,8]{0,1:T(8,128)S(1)} %get-tuple-element.296), channel_id=1, source_target_pairs={{0,4},{4,8},{8,12},{12,16},{16,20},{20,24},{24,28},{28,0},{1,5},{5... | collective-permute-start | bytes 6152 | tf_op jit(solution)/shard_map/ppermute | solution.py:15
  354.1 9.7 %collective-permute-start.36 = (f32[64,34]{0,1:T(8,128)S(1)}, f32[64,34]{0,1:T(8,128)S(1)}, u32[]{:S(2)}, u32[]{:S(2)}) collective-permute-start(f32[64,34]{0,1:T(8,128)S(1)} %get-tuple-element.270), channel_id=1, source_target_pairs={{0,19},{1,20},{2,21},{3,22},{4,23},{5,24},{6,25},{7,26},{8,27},{9,... | collective-permute-start | bytes 26120 | tf_op jit(solution)/shard_map/ppermute | solution.py:15
  354.1 9.7 %collective-permute-start.37 = (f32[64,34]{0,1:T(8,128)S(1)}, f32[64,34]{0,1:T(8,128)S(1)}, u32[]{:S(2)}, u32[]{:S(2)}) collective-permute-start(f32[64,34]{0,1:T(8,128)S(1)} %get-tuple-element.271), channel_id=1, source_target_pairs={{1,0},{2,1},{3,2},{5,4},{6,5},{7,6},{9,8},{10,9},{11,10},{13,12},{... | collective-permute-start | bytes 26120 | tf_op jit(solution)/shard_map/ppermute | solution.py:21
  356.8 7.0 %collective-permute-start.39 = (f32[64,34]{0,1:T(8,128)S(1)}, f32[64,34]{0,1:T(8,128)S(1)}, u32[]{:S(2)}, u32[]{:S(2)}) collective-permute-start(f32[64,34]{0,1:T(8,128)S(1)} %get-tuple-element.269), channel_id=1, source_target_pairs={{0,1},{1,2},{2,3},{4,5},{5,6},{6,7},{8,9},{9,10},{10,11},{12,13},{... | collective-permute-start | bytes 26120 | tf_op jit(solution)/shard_map/ppermute | solution.py:21
  359.9 5.5 collective-permute-start.38
  366.0 4.4 collective-permute-start.40
  370.4 6.6 %collective-permute-start.41 = (f32[64,8]{0,1:T(8,128)}, f32[64,8]{0,1:T(8,128)}, u32[]{:S(2)}, u32[]{:S(2)}) collective-permute-start(f32[64,8]{0,1:T(8,128)} %bitcast.132), channel_id=1, source_target_pairs={{0,4},{4,8},{8,12},{12,16},{16,20},{20,24},{24,28},{28,0},{1,5},{5... | collective-permute-start | bytes 6152 | tf_op jit(solution)/shard_map/ppermute | solution.py:15
  409.0 44.5 %reduce-scatter.8.cloned.1.call-start = ((), (), s32[]{:S(2)}) async-start(), calls=%async_computation.5 | async-start | bytes 327680 | tf_op jit(solution)/shard_map/reduce_scatter | solution.py:174
  411.1 78.3 %reduce-scatter.6.cloned.1.call-start = ((), (), s32[]{:S(2)}) async-start(), calls=%async_computation.3 | async-start | bytes 2949120 | tf_op jit(solution)/shard_map/reduce_scatter | solution.py:173
  415.3 140.5 %all-gather.2.cloned.1.call-start = ((), (), s32[]{:S(2)}) async-start(), calls=%async_computation.4 | async-start | bytes 1474560 | tf_op jit(solution)/shard_map/all_gather | solution.py:179
  417.7 71.8 %copy-start.53 = (f32[64]{0:T(128)S(1)}, f32[64]{0:T(128)}, u32[]{:S(2)}) copy-start(f32[64]{0:T(128)} %get-tuple-element.213) | copy-start | bytes 772
  418.0 124.3 %copy-start.4 = (f32[1,64,256]{1,2,0:T(8,128)S(1)}, f32[1,64,256]{1,2,0:T(8,128)}, u32[]{:S(2)}) copy-start(f32[1,64,256]{1,2,0:T(8,128)} %copy-done.2) | copy-start | bytes 196612
  418.0 124.3 %copy-start.5 = (f32[64,8,32]{0,2,1:T(8,128)S(1)}, f32[64,8,32]{0,2,1:T(8,128)}, u32[]{:S(2)}) copy-start(f32[64,8,32]{0,2,1:T(8,128)} %scatter-add.65) | copy-start | bytes 196612
  418.0 124.3 %copy-start.6 = (f32[64,8,32]{0,2,1:T(8,128)S(1)}, f32[64,8,32]{0,2,1:T(8,128)}, u32[]{:S(2)}) copy-start(f32[64,8,32]{0,2,1:T(8,128)} %scatter-add.71) | copy-start | bytes 196612
  418.0 124.3 %copy-start.26 = (f32[64,8,32]{0,2,1:T(8,128)S(1)}, f32[64,8,32]{0,2,1:T(8,128)}, u32[]{:S(2)}) copy-start(f32[64,8,32]{0,2,1:T(8,128)} %copy-done.25) | copy-start | bytes 196612
  418.1 115.8 %collective-permute-start.42 = (f32[64,34]{0,1:T(8,128)S(1)}, f32[64,34]{0,1:T(8,128)S(1)}, u32[]{:S(2)}, u32[]{:S(2)}) collective-permute-start(f32[64,34]{0,1:T(8,128)S(1)} %get-tuple-element.264), channel_id=1, source_target_pairs={{0,19},{1,20},{2,21},{3,22},{4,23},{5,24},{6,25},{7,26},{8,27},{9,... | collective-permute-start | bytes 26120 | tf_op jit(solution)/shard_map/ppermute | solution.py:15
  418.1 115.8 %collective-permute-start.43 = (f32[64,34]{0,1:T(8,128)S(1)}, f32[64,34]{0,1:T(8,128)S(1)}, u32[]{:S(2)}, u32[]{:S(2)}) collective-permute-start(f32[64,34]{0,1:T(8,128)S(1)} %get-tuple-element.265), channel_id=1, source_target_pairs={{1,0},{2,1},{3,2},{5,4},{6,5},{7,6},{9,8},{10,9},{11,10},{13,12},{... | collective-permute-start | bytes 26120 | tf_op jit(solution)/shard_map/ppermute | solution.py:21
  419.6 114.4 %collective-permute-start.45 = (f32[64,34]{0,1:T(8,128)S(1)}, f32[64,34]{0,1:T(8,128)S(1)}, u32[]{:S(2)}, u32[]{:S(2)}) collective-permute-start(f32[64,34]{0,1:T(8,128)S(1)} %get-tuple-element.263), channel_id=1, source_target_pairs={{0,1},{1,2},{2,3},{4,5},{5,6},{6,7},{8,9},{9,10},{10,11},{12,13},{... | collective-permute-start | bytes 26120 | tf_op jit(solution)/shard_map/ppermute | solution.py:21
  422.6 111.3 %collective-permute-start.44 = (f32[64,34]{0,1:T(8,128)S(1)}, f32[64,34]{0,1:T(8,128)S(1)}, u32[]{:S(2)}, u32[]{:S(2)}) collective-permute-start(f32[64,34]{0,1:T(8,128)S(1)} %get-tuple-element.266), channel_id=1, source_target_pairs={{0,13},{1,14},{2,15},{3,16},{4,17},{5,18},{6,19},{7,20},{8,21},{9,... | collective-permute-start | bytes 26120 | tf_op jit(solution)/shard_map/ppermute | solution.py:15
  534.0 3.7 collective-permute-start.46
  535.8 6.4 %collective-permute-start.47 = (f32[64,8]{0,1:T(8,128)S(1)}, f32[64,8]{0,1:T(8,128)S(1)}, u32[]{:S(2)}, u32[]{:S(2)}) collective-permute-start(f32[64,8]{0,1:T(8,128)S(1)} %bitcast.527), channel_id=1, source_target_pairs={{0,4},{4,8},{8,12},{12,16},{16,20},{20,24},{24,28},{28,0},{1,5},{5... | collective-permute-start | bytes 6152 | tf_op jit(solution)/shard_map/ppermute | solution.py:15
  (46 other events, 434.2 us)
Sparse Core Ops, SparseCore 0:
  409.1 21.2 reduce-scatter.9
  433.5 19.9 reduce-scatter.7
  456.6 32.8 reduce-scatter.5
  534.0 15.9 all-gather.1
